TPU v7x, 32 devices: a whole 2x2x4 slice. The times are simulated.
32 devices in a mesh: fluid: 16 (over z, x, core), solid: 2 (over y).
Axes of the slice: x: 2, y: 2, z: 4, core: 2. Of those that a mesh axis runs over, the one named last changes fastest.
Arguments:
- fluid_load: float32 [2048, 3, 128], P(('fluid', 'solid')), may hold values from -6 to 6
- stiffness: float32 [2048, 3, 128], P(('fluid', 'solid')), may hold values from 0.2 to 2
- mapping: bfloat16 [2048, 128, 128], P(('fluid', 'solid')), may hold values from -0.5 to 0.5
- live_count: int32 [32], P(('fluid', 'solid')), may hold values from 40 to 64, as said below
- dest_device: int32 [2048, 1], P(('fluid', 'solid')), may hold values from 0 to 15; in each aligned block of 64 rows (0 to 63, 64 to 127, ...) at most 8 rows name the same one
- local_block: int32 [2048], P(('fluid', 'solid')), may hold values from 0 to 3
- compliance: float32 [2, 64, 3, 128], P('solid', 'fluid'), may hold values from 0.05 to 0.5
- start_disp: float32 [2, 64, 3, 128], P('solid', 'fluid'), may hold values from -40 to 40
- residual_history: float32 [50, 2, 64, 3, 128], P(None, 'solid', 'fluid'), may hold values from -40 to 40
- update_history: float32 [50, 2, 64, 3, 128], P(None, 'solid', 'fluid'), may hold values from -2.4 to 2.4
Outputs:
- displacement: float32 [2, 64, 3, 128], P('solid', 'fluid')
- fluid_displacement: float32 [2048, 3, 128], P(('fluid', 'solid'))
Inputs may be any that keep to these rules, and one draw needn't show every extreme that they name: `live_count`: each device's live blocks are its first ones; some device has exactly 64. `dest_device`: among the 64 rows of one device no fluid index appears more than 8 times.
All inputs are finite; a program needn't handle non-finite values.
Results may differ from a plain program's by a relative error of at most 0.0094.
Values may be sent and summed in bfloat16 or wider, within the bound.
A program may use at most 64 MiB of HBM per device.

v0:
```python
import jax
import jax.numpy as jnp
from jax import lax
from jax.sharding import PartitionSpec as P

ITERS = 2
ridge_share = 0.01


def solve_small(gram_matrix, right_side):
    order = gram_matrix.shape[0]
    ridge = ridge_share * jnp.trace(gram_matrix) / order
    factor = jnp.linalg.cholesky(gram_matrix + ridge * jnp.eye(order, dtype=gram_matrix.dtype))
    halfway = lax.linalg.triangular_solve(factor, right_side[:, None], left_side=True, lower=True)
    solved = lax.linalg.triangular_solve(
        factor, halfway, left_side=True, lower=True, transpose_a=True
    )
    return -solved[:, 0]


def full_sums(basis_flat, resid_flat):
    gram_local = jnp.dot(basis_flat, basis_flat.T, precision=lax.Precision.HIGHEST)
    right_local = jnp.dot(basis_flat, resid_flat, precision=lax.Precision.HIGHEST)
    return lax.psum((gram_local, right_local), ("fluid", "solid"))


def body(
    fluid_load,
    stiffness,
    mapping,
    live_count,
    dest_device,
    local_block,
    compliance,
    start_disp,
    residual_history,
    update_history,
):
    blocks = mapping.shape[0]
    struct_width = mapping.shape[1]
    sub_blocks = compliance.shape[1]
    fluid_size = lax.axis_size("fluid")
    alive = (jnp.arange(blocks) < live_count[0]).astype(jnp.float32)[:, None, None]
    capacity = max(2, 2 * ((blocks + fluid_size - 1) // fluid_size))
    dest_hot = (dest_device[:, 0][:, None] == jnp.arange(fluid_size)[None, :]).astype(jnp.int32)
    slot_rank = jnp.sum((jnp.cumsum(dest_hot, axis=0) - 1) * dest_hot, axis=1)
    slot_index = dest_device[:, 0] * capacity + slot_rank
    slot_hot = jnp.arange(fluid_size * capacity)[:, None] == slot_index[None, :]
    sent_ids = jnp.sum(slot_hot.astype(jnp.int32) * (local_block + 1)[None, :], axis=1) - 1
    owner_ids = lax.all_to_all(
        sent_ids.reshape(fluid_size, capacity), "fluid", split_axis=0, concat_axis=0, tiled=True
    )
    owner_hot = owner_ids.reshape(-1)[None, :] == jnp.arange(sub_blocks)[:, None]

    def to_fluid(struct_disp):
        packed = struct_disp[0].astype(jnp.bfloat16)
        chosen = jnp.einsum(
            "ks,kcj->scj",
            owner_hot.astype(jnp.bfloat16),
            packed,
            preferred_element_type=jnp.float32,
        ).astype(jnp.bfloat16)
        returned = lax.all_to_all(
            chosen.reshape(fluid_size, capacity, 3, struct_width),
            "fluid",
            split_axis=0,
            concat_axis=0,
            tiled=True,
        )
        picked = jnp.einsum(
            "sb,scj->bcj",
            slot_hot.astype(jnp.bfloat16),
            returned.reshape(-1, 3, struct_width),
            preferred_element_type=jnp.float32,
        )
        fluid_disp = jnp.einsum(
            "bjn,bcj->bcn", mapping, picked.astype(jnp.bfloat16), preferred_element_type=jnp.float32
        )
        return fluid_disp * alive

    struct_disp = start_disp
    basis_cols = residual_history
    updates = update_history
    last_resid = struct_disp
    last_image = struct_disp
    gram_matrix = None
    for iteration in range(ITERS):
        fluid_disp = to_fluid(struct_disp)
        fluid_force = (alive * (fluid_load - stiffness * fluid_disp)).astype(jnp.bfloat16)
        contrib = jnp.einsum(
            "bjn,bcn->bcj", mapping, fluid_force, preferred_element_type=jnp.float32
        )
        buffer = jnp.einsum(
            "sb,bcj->scj", slot_hot.astype(jnp.float32), contrib, precision=lax.Precision.HIGHEST
        )
        received = lax.all_to_all(
            buffer.reshape(fluid_size, capacity, 3, struct_width),
            "fluid",
            split_axis=0,
            concat_axis=0,
            tiled=True,
        )
        summed = jnp.einsum(
            "ks,scj->kcj",
            owner_hot.astype(jnp.float32),
            received.reshape(-1, 3, struct_width),
            precision=lax.Precision.HIGHEST,
        )
        struct_image = compliance * summed[None]
        residual = struct_image - struct_disp
        newest = residual - last_resid
        if iteration > 0:
            basis_cols = jnp.concatenate([basis_cols[1:], newest[None]], 0)
            updates = jnp.concatenate([updates[1:], (struct_image - last_image)[None]], 0)
        basis_flat = basis_cols.reshape(basis_cols.shape[0], -1)
        resid_flat = residual.reshape(-1)
        gram_matrix, right_side = full_sums(basis_flat, resid_flat)
        coefficients = solve_small(gram_matrix, right_side)
        struct_disp = struct_image + jnp.tensordot(
            coefficients, updates, axes=1, precision=lax.Precision.HIGHEST
        )
        last_resid = residual
        last_image = struct_image
    final_disp = to_fluid(struct_disp)
    return (struct_disp, final_disp)


def solution(mesh):
    in_specs = (
        P(("fluid", "solid"), None, None),
        P(("fluid", "solid"), None, None),
        P(("fluid", "solid"), None, None),
        P(("fluid", "solid")),
        P(("fluid", "solid"), None),
        P(("fluid", "solid")),
        P("solid", "fluid", None, None),
        P("solid", "fluid", None, None),
        P(None, "solid", "fluid", None, None),
        P(None, "solid", "fluid", None, None),
    )
    out_specs = (P("solid", "fluid", None, None), P(("fluid", "solid"), None, None))
    return jax.shard_map(body, mesh=mesh, in_specs=in_specs, out_specs=out_specs, check_vma=False)
```

profile of v0, /device:TPU:0, one launch (start us, length us, event | category | flops | bytes accessed | tf_op | source)
XLA Modules:
  0.0 190.6 jit_solution(16942165006575213732)
XLA Ops:
  0.6 0.0 copy-start
  0.6 0.9 fusion.48
  1.5 0.1 reduce_window_sum.11
  1.6 0.8 select_reduce_fusion.1
  2.5 0.7 multiply_add_fusion
  3.1 0.1 select_reduce_fusion
  3.2 0.1 sub.30
  3.3 13.6 %all_to_all.31 = s32[16,1,8]{2,1,0:T(1,128)S(1)} all-to-all(s32[16,1,8]{2,1,0:T(1,128)S(1)} %bitcast.179), channel_id=1, replica_groups=mesh['fluid'=16,'solid'=2] {'fluid'}, dimensions={0} | all-to-all | bytes 1024 | tf_op jit(solution)/shard_map/all_to_all | solution.py:50
  17.0 0.5 broadcast.90
  17.5 0.7 reduce.7
  18.1 0.1 eq.60
  18.2 0.9 fusion.8
  19.2 0.7 copy.39
  19.8 3.5 %all-to-all-start.1 = ((bf16[16,8,3,128]{3,1,2,0:T(8,128)(2,1)}), bf16[16,8,3,128]{3,1,2,0:T(8,128)(2,1)S(1)}, u32[]{:S(2)}, u32[]{:S(2)}) async-start(bf16[16,8,3,128]{3,1,2,0:T(8,128)(2,1)} %copy.39), calls=%async_computation.1 | async-start | bytes 196608 | tf_op jit(solution)/shard_map/all_to_all | solution.py:63
  24.0 6.7 %all-to-all-done.1 = bf16[16,8,3,128]{3,1,2,0:T(8,128)(2,1)S(1)} async-done(((bf16[16,8,3,128]{3,1,2,0:T(8,128)(2,1)}), bf16[16,8,3,128]{3,1,2,0:T(8,128)(2,1)S(1)}, u32[]{:S(2)}, u32[]{:S(2)}) %all-to-all-start.1) | async-done | bytes 98336 | tf_op jit(solution)/shard_map/all_to_all | solution.py:63
  30.7 0.2 convolution_convert_fusion.5
  30.9 0.0 copy-start.1
  30.9 0.0 copy-start.5
  30.9 0.0 copy-start.6
  30.9 2.7 %fusion.12 = f32[64,3,128]{2,1,0:T(4,128)S(1)} fusion(bf16[64,128,128]{2,1,0:T(8,128)(2,1)S(1)} %copy-done, f32[64,3,128]{2,0,1:T(8,128)} %param.15, f32[64,3,128]{2,0,1:T(8,128)} %param.16, bf16[64,3,128]{2,0,1:T(8,128)(2,1)S(1)} %convolution_convert_fusion.5, f32[64]{0:T(128)S(1)} %compare_convert_fusion), kind=kOutput, calls=%fused_computation.23 | convolution fusion | flops 12705792 | bytes 2441472 | tf_op jit(solution)/shard_map/bjn,bcn->bcj/dot_general | solution.py:90
  33.7 0.4 convolution_bitcast_fusion.1
  34.0 0.7 copy.45
  34.7 3.5 %all-to-all-start.2 = ((f32[16,8,3,128]{3,1,2,0:T(8,128)}), f32[16,8,3,128]{3,1,2,0:T(8,128)S(1)}, u32[]{:S(2)}, u32[]{:S(2)}) async-start(f32[16,8,3,128]{3,1,2,0:T(8,128)} %copy.45), calls=%async_computation.2 | async-start | bytes 393216 | tf_op jit(solution)/shard_map/all_to_all | solution.py:96
  38.3 0.4 convolution_bitcast_fusion.3
  38.7 8.5 %all-to-all-done.2 = f32[16,8,3,128]{3,1,2,0:T(8,128)S(1)} async-done(((f32[16,8,3,128]{3,1,2,0:T(8,128)}), f32[16,8,3,128]{3,1,2,0:T(8,128)S(1)}, u32[]{:S(2)}, u32[]{:S(2)}) %all-to-all-start.2) | async-done | bytes 196640 | tf_op jit(solution)/shard_map/all_to_all | solution.py:96
  47.2 0.2 fusion.84
  47.4 0.4 convolution_bitcast_fusion.7
  47.7 37.9 %all-reduce.1 = (f32[50,1]{0,1:T(1,128)S(1)}, f32[50,50]{0,1:T(8,128)S(1)}) all-reduce(f32[50,1]{0,1:T(1,128)S(1)} %convolution_bitcast_fusion.7, f32[50,50]{0,1:T(8,128)S(1)} %convolution_bitcast_fusion.3), channel_id=1, replica_groups=mesh['fluid'=16,'solid'=2] {'fluid','solid'}, use_global_device_ids=true, to_apply=%region_7.9 | all-reduce | flops 2550 | bytes 20400 | tf_op jit(solution)/shard_map/psum | solution.py:24
  85.6 0.6 select_reduce_fusion.5
  86.9 0.1 copy.50
  87.0 4.6 %cholesky.44 = f32[50,50]{1,0:T(8,128)S(1)} custom-call(f32[50,50]{1,0:T(8,128)S(1)} %fusion.62), custom_call_target="Cholesky" | custom-call | tf_op jit(solution)/shard_map/jit(cholesky)/cholesky | solution.py:13
  91.6 0.6 compare_reduce_fusion.1
  92.3 0.7 fusion.55
  92.9 3.8 %custom-call.11 = f32[1,50,50]{1,2,0:T(8,128)S(1)} custom-call(f32[1,50,50]{2,1,0:T(8,128)S(1)} %fusion.55), custom_call_target="InvertDiagBlocksLowerTriangular" | custom-call | tf_op jit(solution)/shard_map/triangular_solve/custom-call.2 | solution.py:15
  96.8 0.2 convolution_bitcast_fusion.11
  96.9 0.2 fusion.18
  97.1 0.3 fusion.21
  97.4 0.3 fusion.9
  97.7 12.5 %all_to_all.32 = bf16[16,8,3,128]{3,1,2,0:T(8,128)(2,1)S(1)} all-to-all(bf16[16,8,3,128]{3,1,2,0:T(8,128)(2,1)S(1)} %copy.51), channel_id=1, replica_groups=mesh['fluid'=16,'solid'=2] {'fluid'}, dimensions={0} | all-to-all | bytes 196608 | tf_op jit(solution)/shard_map/all_to_all | solution.py:63
  110.1 0.2 convolution_convert_fusion.4
  110.4 1.7 fusion.11
  112.1 0.4 convolution_bitcast_fusion
  112.5 0.7 copy.57
  113.2 3.5 %all-to-all-start.4 = ((f32[16,8,3,128]{3,1,2,0:T(8,128)}), f32[16,8,3,128]{3,1,2,0:T(8,128)S(1)}, u32[]{:S(2)}, u32[]{:S(2)}) async-start(f32[16,8,3,128]{3,1,2,0:T(8,128)} %copy.57), calls=%async_computation.4 | async-start | bytes 393216 | tf_op jit(solution)/shard_map/all_to_all | solution.py:96
  116.8 8.8 %all-to-all-done.4 = f32[16,8,3,128]{3,1,2,0:T(8,128)S(1)} async-done(((f32[16,8,3,128]{3,1,2,0:T(8,128)}), f32[16,8,3,128]{3,1,2,0:T(8,128)S(1)}, u32[]{:S(2)}, u32[]{:S(2)}) %all-to-all-start.4) | async-done | bytes 196640 | tf_op jit(solution)/shard_map/all_to_all | solution.py:96
  125.6 0.2 fusion.13
  125.8 0.4 convolution_bitcast_fusion.2
  126.3 0.4 convolution_bitcast_fusion.6
  126.6 37.9 %all-reduce = (f32[50,1]{0,1:T(1,128)S(1)}, f32[50,50]{0,1:T(8,128)S(1)}) all-reduce(f32[50,1]{0,1:T(1,128)S(1)} %convolution_bitcast_fusion.6, f32[50,50]{0,1:T(8,128)S(1)} %convolution_bitcast_fusion.2), channel_id=1, replica_groups=mesh['fluid'=16,'solid'=2] {'fluid','solid'}, use_global_device_ids=true, to_apply=%region_10.14 | all-reduce | flops 2550 | bytes 20400 | tf_op jit(solution)/shard_map/psum | solution.py:24
  164.5 0.6 select_reduce_fusion.4
  165.8 0.1 copy.62
  165.9 4.6 %cholesky.55 = f32[50,50]{1,0:T(8,128)S(1)} custom-call(f32[50,50]{1,0:T(8,128)S(1)} %fusion.59), custom_call_target="Cholesky" | custom-call | tf_op jit(solution)/shard_map/jit(cholesky)/cholesky | solution.py:13
  170.5 0.6 compare_reduce_fusion
  171.2 0.7 fusion.56
  171.8 3.8 %custom-call.13 = f32[1,50,50]{1,2,0:T(8,128)S(1)} custom-call(f32[1,50,50]{2,1,0:T(8,128)S(1)} %fusion.56), custom_call_target="InvertDiagBlocksLowerTriangular" | custom-call | tf_op jit(solution)/shard_map/triangular_solve/custom-call.2 | solution.py:15
  175.6 0.2 convolution_bitcast_fusion.9
  175.8 0.2 fusion.16
  176.0 0.1 maximum_bitcast_fusion.1
  176.0 0.3 fusion.19
  176.4 0.3 fusion.10
  176.6 12.5 %all_to_all.33 = bf16[16,8,3,128]{3,1,2,0:T(8,128)(2,1)S(1)} all-to-all(bf16[16,8,3,128]{3,1,2,0:T(8,128)(2,1)S(1)} %copy.63), channel_id=1, replica_groups=mesh['fluid'=16,'solid'=2] {'fluid'}, dimensions={0} | all-to-all | bytes 196608 | tf_op jit(solution)/shard_map/all_to_all | solution.py:63
  189.1 0.2 convolution_convert_fusion.3
  189.3 0.6 convolution_multiply_fusion
  190.0 0.7 copy.66
  (28 shorter events, 0.3 us)
Async XLA Ops:
  0.6 30.3 %copy-start = (bf16[64,128,128]{2,1,0:T(8,128)(2,1)S(1)}, bf16[64,128,128]{2,1,0:T(8,128)(2,1)}, u32[]{:S(2)}) copy-start(bf16[64,128,128]{2,1,0:T(8,128)(2,1)} %param.17) | copy-start | bytes 6291460
  19.8 10.9 %all-to-all-start.1 = ((bf16[16,8,3,128]{3,1,2,0:T(8,128)(2,1)}), bf16[16,8,3,128]{3,1,2,0:T(8,128)(2,1)S(1)}, u32[]{:S(2)}, u32[]{:S(2)}) async-start(bf16[16,8,3,128]{3,1,2,0:T(8,128)(2,1)} %copy.39), calls=%async_computation.1 | async-start | bytes 196608 | tf_op jit(solution)/shard_map/all_to_all | solution.py:63
  30.9 7.3 %copy-start.1 = (f32[50,1,4,3,128]{4,2,3,1,0:T(4,128)S(1)}, f32[50,1,4,3,128]{4,2,3,1,0:T(4,128)}, u32[]{:S(2)}) copy-start(f32[50,1,4,3,128]{4,2,3,1,0:T(4,128)} %param.23) | copy-start | bytes 921604
  30.9 16.3 %copy-start.5 = (f32[1,4,3,128]{3,1,2,0:T(4,128)S(1)}, f32[1,4,3,128]{3,1,2,0:T(4,128)}, u32[]{:S(2)}) copy-start(f32[1,4,3,128]{3,1,2,0:T(4,128)} %param.21) | copy-start | bytes 18436
  30.9 16.3 %copy-start.6 = (f32[1,4,3,128]{3,1,2,0:T(4,128)S(1)}, f32[1,4,3,128]{3,1,2,0:T(4,128)}, u32[]{:S(2)}) copy-start(f32[1,4,3,128]{3,1,2,0:T(4,128)} %param.22) | copy-start | bytes 18436
  33.6 63.4 %copy-start.2 = (f32[50,1,4,3,128]{4,2,3,1,0:T(4,128)S(1)}, f32[50,1,4,3,128]{4,2,3,1,0:T(4,128)}, u32[]{:S(2)}) copy-start(f32[50,1,4,3,128]{4,2,3,1,0:T(4,128)} %param.24) | copy-start | bytes 921604
  33.6 76.7 %copy-start.3 = (f32[64,3,128]{2,0,1:T(8,128)S(1)}, f32[64,3,128]{2,0,1:T(8,128)}, u32[]{:S(2)}) copy-start(f32[64,3,128]{2,0,1:T(8,128)} %param.15) | copy-start | bytes 294916
  33.6 76.7 %copy-start.4 = (f32[64,3,128]{2,0,1:T(8,128)S(1)}, f32[64,3,128]{2,0,1:T(8,128)}, u32[]{:S(2)}) copy-start(f32[64,3,128]{2,0,1:T(8,128)} %param.16) | copy-start | bytes 294916
  34.7 12.5 %all-to-all-start.2 = ((f32[16,8,3,128]{3,1,2,0:T(8,128)}), f32[16,8,3,128]{3,1,2,0:T(8,128)S(1)}, u32[]{:S(2)}, u32[]{:S(2)}) async-start(f32[16,8,3,128]{3,1,2,0:T(8,128)} %copy.45), calls=%async_computation.2 | async-start | bytes 393216 | tf_op jit(solution)/shard_map/all_to_all | solution.py:96
  113.2 12.5 %all-to-all-start.4 = ((f32[16,8,3,128]{3,1,2,0:T(8,128)}), f32[16,8,3,128]{3,1,2,0:T(8,128)S(1)}, u32[]{:S(2)}, u32[]{:S(2)}) async-start(f32[16,8,3,128]{3,1,2,0:T(8,128)} %copy.57), calls=%async_computation.4 | async-start | bytes 393216 | tf_op jit(solution)/shard_map/all_to_all | solution.py:96
  176.3 14.3 %copy-start.7 = (f32[1,4,3,128]{3,1,2,0:T(4,128)}, f32[1,4,3,128]{3,1,2,0:T(4,128)S(1)}, u32[]{:S(2)}) copy-start(f32[1,4,3,128]{3,1,2,0:T(4,128)S(1)} %copy_add_fusion) | copy-start | bytes 18436
where the time goes:
time: 192 us; the launch traced here: 191 us
  blocking collectives  114 us (59%)
  other arithmetic  24.1 us (13%)
  waiting for transfers between devices  24 us (12%)
  matrix products  11 us (6%)
  starting transfers between devices  10.5 us (5%)
  local copies, waits for them, and re-layouts  3.73 us (2%)
  between operations  2.92 us (2%)
    psum x2, blocking collectives, full_sums(): return lax.psum((gram_local, right_local), ('fluid', 'solid'))  75.8 us
    all_to_all x2, blocking collectives, to_fluid(): lax.all_to_all(chosen.reshape(fluid_size, capacity, 3, struct_width), 'fl...  24.9 us
    all_to_all x2, waiting for transfers between devices, body(): lax.all_to_all(buffer.reshape(fluid_size, capacity, 3, struct_width), 'fl...  17.3 us
    all_to_all x1, blocking collectives, body(): lax.all_to_all(sent_ids.reshape(fluid_size, capacity), 'fluid', split_axi...  13.6 us
    another operation x6, other arithmetic, solve_small(): jnp.linalg.cholesky(gram_matrix + ridge * jnp.eye(order, dtype=gram_matri...  10.5 us
    another operation x4, other arithmetic, solve_small(): lax.linalg.triangular_solve(factor, halfway, left_side=True, lower=True,...  8.96 us
    all_to_all x2, starting transfers between devices, body(): lax.all_to_all(buffer.reshape(fluid_size, capacity, 3, struct_width), 'fl...  7.04 us
    all_to_all x1, waiting for transfers between devices, to_fluid(): lax.all_to_all(chosen.reshape(fluid_size, capacity, 3, struct_width), 'fl...  6.69 us
  transfers between devices with their start and end apart: 3, of which 3 were waited for; matrix products, arithmetic and copies ran while one was open for 0% of the time, Pallas kernels for 0%

commit v1 on v0

--- a/solution.py
+++ b/solution.py
@@ -5,6 +5,11 @@
 
 ITERS = 2
 ridge_share = 0.01
+
+
+def axis_by_axis(array, first, second):
+    inner = lax.psum(array, first)
+    return lax.psum(inner, second)
 
 
 def solve_small(gram_matrix, right_side):
@@ -21,7 +26,7 @@
 def full_sums(basis_flat, resid_flat):
     gram_local = jnp.dot(basis_flat, basis_flat.T, precision=lax.Precision.HIGHEST)
     right_local = jnp.dot(basis_flat, resid_flat, precision=lax.Precision.HIGHEST)
-    return lax.psum((gram_local, right_local), ("fluid", "solid"))
+    return axis_by_axis((gram_local, right_local), "solid", "fluid")
 
 
 def body(

time: 192 us -> 242 us (1.26)
  blocking collectives: 114 us -> 165 us
    psum x2 -> x4, blocking collectives: 75.8 us -> 131 us  [the longest x2 115 us: axis_by_axis(): return lax.psum(inner, second)]
    all_to_all x2, blocking collectives: 24.9 us -> 19.9 us  [to_fluid(): lax.all_to_all(chosen.reshape(fluid_size, capacity, 3, struct_width), 'fl...]
where the time goes in v1:
time: 242 us; the launch traced here: 241 us
  blocking collectives  165 us (68%)
  other arithmetic  24.1 us (10%)
  waiting for transfers between devices  24 us (10%)
  matrix products  11 us (5%)
  starting transfers between devices  10.5 us (4%)
  local copies, waits for them, and re-layouts  3.73 us (2%)
  between operations  2.91 us (1%)
    psum x2, blocking collectives, axis_by_axis(): return lax.psum(inner, second)  115 us
    all_to_all x2, blocking collectives, to_fluid(): lax.all_to_all(chosen.reshape(fluid_size, capacity, 3, struct_width), 'fl...  19.9 us
    all_to_all x2, waiting for transfers between devices, body(): lax.all_to_all(buffer.reshape(fluid_size, capacity, 3, struct_width), 'fl...  17.3 us
    psum x2, blocking collectives, axis_by_axis(): inner = lax.psum(array, first)  15.8 us
    all_to_all x1, blocking collectives, body(): lax.all_to_all(sent_ids.reshape(fluid_size, capacity), 'fluid', split_axi...  13.6 us
    another operation x6, other arithmetic, solve_small(): jnp.linalg.cholesky(gram_matrix + ridge * jnp.eye(order, dtype=gram_matri...  10.5 us
    another operation x4, other arithmetic, solve_small(): lax.linalg.triangular_solve(factor, halfway, left_side=True, lower=True,...  8.96 us
    all_to_all x2, starting transfers between devices, body(): lax.all_to_all(buffer.reshape(fluid_size, capacity, 3, struct_width), 'fl...  7.04 us
  transfers between devices with their start and end apart: 3, of which 3 were waited for; matrix products, arithmetic and copies ran while one was open for 0% of the time, Pallas kernels for 0%

profile of v1, /device:TPU:0, one launch (start us, length us, event | category | flops | bytes accessed | tf_op | source)
XLA Modules:
  0.0 240.9 jit_solution(5126716466400699133)
XLA Ops:
  0.6 0.0 copy-start
  0.6 0.9 fusion.48
  1.5 0.1 reduce_window_sum.11
  1.6 0.8 select_reduce_fusion.1
  2.5 0.7 multiply_add_fusion
  3.1 0.1 select_reduce_fusion
  3.2 0.1 sub.30
  3.3 13.6 %all_to_all.31 = s32[16,1,8]{2,1,0:T(1,128)S(1)} all-to-all(s32[16,1,8]{2,1,0:T(1,128)S(1)} %bitcast.177), channel_id=1, replica_groups=mesh['fluid'=16,'solid'=2] {'fluid'}, dimensions={0} | all-to-all | bytes 1024 | tf_op jit(solution)/shard_map/all_to_all | solution.py:55
  17.0 0.5 broadcast.90
  17.5 0.7 reduce.7
  18.1 0.1 eq.60
  18.2 0.9 fusion.8
  19.2 0.7 copy.39
  19.8 3.5 %all-to-all-start.1 = ((bf16[16,8,3,128]{3,1,2,0:T(8,128)(2,1)}), bf16[16,8,3,128]{3,1,2,0:T(8,128)(2,1)S(1)}, u32[]{:S(2)}, u32[]{:S(2)}) async-start(bf16[16,8,3,128]{3,1,2,0:T(8,128)(2,1)} %copy.39), calls=%async_computation.1 | async-start | bytes 196608 | tf_op jit(solution)/shard_map/all_to_all | solution.py:68
  24.0 6.7 %all-to-all-done.1 = bf16[16,8,3,128]{3,1,2,0:T(8,128)(2,1)S(1)} async-done(((bf16[16,8,3,128]{3,1,2,0:T(8,128)(2,1)}), bf16[16,8,3,128]{3,1,2,0:T(8,128)(2,1)S(1)}, u32[]{:S(2)}, u32[]{:S(2)}) %all-to-all-start.1) | async-done | bytes 98336 | tf_op jit(solution)/shard_map/all_to_all | solution.py:68
  30.7 0.2 convolution_convert_fusion.5
  30.9 0.0 copy-start.1
  30.9 2.7 %fusion.12 = f32[64,3,128]{2,1,0:T(4,128)S(1)} fusion(bf16[64,128,128]{2,1,0:T(8,128)(2,1)S(1)} %copy-done, f32[64,3,128]{2,0,1:T(8,128)} %param.15, f32[64,3,128]{2,0,1:T(8,128)} %param.16, bf16[64,3,128]{2,0,1:T(8,128)(2,1)S(1)} %convolution_convert_fusion.5, f32[64]{0:T(128)S(1)} %compare_convert_fusion), kind=kOutput, calls=%fused_computation.23 | convolution fusion | flops 12705792 | bytes 2441472 | tf_op jit(solution)/shard_map/bjn,bcn->bcj/dot_general | solution.py:95
  33.7 0.4 convolution_bitcast_fusion.1
  34.0 0.7 copy.45
  34.7 3.5 %all-to-all-start.2 = ((f32[16,8,3,128]{3,1,2,0:T(8,128)}), f32[16,8,3,128]{3,1,2,0:T(8,128)S(1)}, u32[]{:S(2)}, u32[]{:S(2)}) async-start(f32[16,8,3,128]{3,1,2,0:T(8,128)} %copy.45), calls=%async_computation.2 | async-start | bytes 393216 | tf_op jit(solution)/shard_map/all_to_all | solution.py:101
  38.3 0.4 convolution_bitcast_fusion.3
  38.7 8.5 %all-to-all-done.2 = f32[16,8,3,128]{3,1,2,0:T(8,128)S(1)} async-done(((f32[16,8,3,128]{3,1,2,0:T(8,128)}), f32[16,8,3,128]{3,1,2,0:T(8,128)S(1)}, u32[]{:S(2)}, u32[]{:S(2)}) %all-to-all-start.2) | async-done | bytes 196640 | tf_op jit(solution)/shard_map/all_to_all | solution.py:101
  47.2 0.2 fusion.84
  47.4 0.4 convolution_bitcast_fusion.7
  47.7 8.4 %all-reduce.3 = (f32[50]{0:T(128)S(1)}, f32[50,50]{0,1:T(8,128)S(1)}) all-reduce(f32[50]{0:T(128)S(1)} %convolution_bitcast_fusion.7, f32[50,50]{0,1:T(8,128)S(1)} %convolution_bitcast_fusion.3), channel_id=1, replica_groups=mesh['fluid'=16,'solid'=2] {'solid'}, use_global_device_ids=true, to_apply=%region_8.10 | all-reduce | flops 2550 | bytes 20400 | tf_op jit(solution)/shard_map/psum | solution.py:11
  56.1 57.7 %all-reduce.1 = (f32[50,1]{0,1:T(1,128)S(1)}, f32[50,50]{0,1:T(8,128)S(1)}) all-reduce(f32[50,1]{0,1:T(1,128)S(1)} %bitcast.180, f32[50,50]{0,1:T(8,128)S(1)} %get-tuple-element.18), channel_id=1, replica_groups=mesh['fluid'=16,'solid'=2] {'fluid'}, use_global_device_ids=true, to_apply=%region_9.11 | all-reduce | flops 2550 | bytes 20400 | tf_op jit(solution)/shard_map/psum | solution.py:12
  113.8 0.6 select_reduce_fusion.5
  115.1 0.1 copy.50
  115.2 4.6 %cholesky.44 = f32[50,50]{1,0:T(8,128)S(1)} custom-call(f32[50,50]{1,0:T(8,128)S(1)} %fusion.62), custom_call_target="Cholesky" | custom-call | tf_op jit(solution)/shard_map/jit(cholesky)/cholesky | solution.py:18
  119.8 0.6 compare_reduce_fusion.1
  120.4 0.7 fusion.55
  121.1 3.8 %custom-call.11 = f32[1,50,50]{1,2,0:T(8,128)S(1)} custom-call(f32[1,50,50]{2,1,0:T(8,128)S(1)} %fusion.55), custom_call_target="InvertDiagBlocksLowerTriangular" | custom-call | tf_op jit(solution)/shard_map/triangular_solve/custom-call.2 | solution.py:20
  124.9 0.2 convolution_bitcast_fusion.11
  125.1 0.2 fusion.18
  125.2 0.3 fusion.21
  125.6 0.3 fusion.9
  125.8 10.0 %all_to_all.32 = bf16[16,8,3,128]{3,1,2,0:T(8,128)(2,1)S(1)} all-to-all(bf16[16,8,3,128]{3,1,2,0:T(8,128)(2,1)S(1)} %copy.51), channel_id=1, replica_groups=mesh['fluid'=16,'solid'=2] {'fluid'}, dimensions={0} | all-to-all | bytes 196608 | tf_op jit(solution)/shard_map/all_to_all | solution.py:68
  135.8 0.2 convolution_convert_fusion.4
  136.0 1.7 fusion.11
  137.8 0.4 convolution_bitcast_fusion
  138.1 0.7 copy.57
  138.8 3.5 %all-to-all-start.4 = ((f32[16,8,3,128]{3,1,2,0:T(8,128)}), f32[16,8,3,128]{3,1,2,0:T(8,128)S(1)}, u32[]{:S(2)}, u32[]{:S(2)}) async-start(f32[16,8,3,128]{3,1,2,0:T(8,128)} %copy.57), calls=%async_computation.4 | async-start | bytes 393216 | tf_op jit(solution)/shard_map/all_to_all | solution.py:101
  142.5 8.8 %all-to-all-done.4 = f32[16,8,3,128]{3,1,2,0:T(8,128)S(1)} async-done(((f32[16,8,3,128]{3,1,2,0:T(8,128)}), f32[16,8,3,128]{3,1,2,0:T(8,128)S(1)}, u32[]{:S(2)}, u32[]{:S(2)}) %all-to-all-start.4) | async-done | bytes 196640 | tf_op jit(solution)/shard_map/all_to_all | solution.py:101
  151.3 0.2 fusion.13
  151.5 0.4 convolution_bitcast_fusion.2
  151.9 0.4 convolution_bitcast_fusion.6
  152.3 7.4 %all-reduce.2 = (f32[50]{0:T(128)S(1)}, f32[50,50]{0,1:T(8,128)S(1)}) all-reduce(f32[50]{0:T(128)S(1)} %convolution_bitcast_fusion.6, f32[50,50]{0,1:T(8,128)S(1)} %convolution_bitcast_fusion.2), channel_id=1, replica_groups=mesh['fluid'=16,'solid'=2] {'solid'}, use_global_device_ids=true, to_apply=%region_13.17 | all-reduce | flops 2550 | bytes 20400 | tf_op jit(solution)/shard_map/psum | solution.py:11
  159.7 57.7 %all-reduce = (f32[50,1]{0,1:T(1,128)S(1)}, f32[50,50]{0,1:T(8,128)S(1)}) all-reduce(f32[50,1]{0,1:T(1,128)S(1)} %bitcast.181, f32[50,50]{0,1:T(8,128)S(1)} %get-tuple-element.16), channel_id=1, replica_groups=mesh['fluid'=16,'solid'=2] {'fluid'}, use_global_device_ids=true, to_apply=%region_14.18 | all-reduce | flops 2550 | bytes 20400 | tf_op jit(solution)/shard_map/psum | solution.py:12
  217.3 0.6 select_reduce_fusion.4
  218.6 0.1 copy.62
  218.7 4.6 %cholesky.55 = f32[50,50]{1,0:T(8,128)S(1)} custom-call(f32[50,50]{1,0:T(8,128)S(1)} %fusion.59), custom_call_target="Cholesky" | custom-call | tf_op jit(solution)/shard_map/jit(cholesky)/cholesky | solution.py:18
  223.3 0.6 compare_reduce_fusion
  224.0 0.7 fusion.56
  224.6 3.8 %custom-call.13 = f32[1,50,50]{1,2,0:T(8,128)S(1)} custom-call(f32[1,50,50]{2,1,0:T(8,128)S(1)} %fusion.56), custom_call_target="InvertDiagBlocksLowerTriangular" | custom-call | tf_op jit(solution)/shard_map/triangular_solve/custom-call.2 | solution.py:20
  228.5 0.2 convolution_bitcast_fusion.9
  228.6 0.2 fusion.16
  228.8 0.1 maximum_bitcast_fusion.1
  228.9 0.3 fusion.19
  229.2 0.3 fusion.10
  229.5 10.0 %all_to_all.33 = bf16[16,8,3,128]{3,1,2,0:T(8,128)(2,1)S(1)} all-to-all(bf16[16,8,3,128]{3,1,2,0:T(8,128)(2,1)S(1)} %copy.63), channel_id=1, replica_groups=mesh['fluid'=16,'solid'=2] {'fluid'}, dimensions={0} | all-to-all | bytes 196608 | tf_op jit(solution)/shard_map/all_to_all | solution.py:68
  239.4 0.2 convolution_convert_fusion.3
  239.6 0.6 convolution_multiply_fusion
  240.3 0.7 copy.66
  (30 shorter events, 0.3 us)
Async XLA Ops:
  0.6 30.3 %copy-start = (bf16[64,128,128]{2,1,0:T(8,128)(2,1)S(1)}, bf16[64,128,128]{2,1,0:T(8,128)(2,1)}, u32[]{:S(2)}) copy-start(bf16[64,128,128]{2,1,0:T(8,128)(2,1)} %param.17) | copy-start | bytes 6291460
  19.8 10.9 %all-to-all-start.1 = ((bf16[16,8,3,128]{3,1,2,0:T(8,128)(2,1)}), bf16[16,8,3,128]{3,1,2,0:T(8,128)(2,1)S(1)}, u32[]{:S(2)}, u32[]{:S(2)}) async-start(bf16[16,8,3,128]{3,1,2,0:T(8,128)(2,1)} %copy.39), calls=%async_computation.1 | async-start | bytes 196608 | tf_op jit(solution)/shard_map/all_to_all | solution.py:68
  30.9 7.3 %copy-start.1 = (f32[50,1,4,3,128]{4,2,3,1,0:T(4,128)S(1)}, f32[50,1,4,3,128]{4,2,3,1,0:T(4,128)}, u32[]{:S(2)}) copy-start(f32[50,1,4,3,128]{4,2,3,1,0:T(4,128)} %param.23) | copy-start | bytes 921604
  30.9 16.3 %copy-start.5 = (f32[1,4,3,128]{3,1,2,0:T(4,128)S(1)}, f32[1,4,3,128]{3,1,2,0:T(4,128)}, u32[]{:S(2)}) copy-start(f32[1,4,3,128]{3,1,2,0:T(4,128)} %param.21) | copy-start | bytes 18436
  30.9 16.3 %copy-start.6 = (f32[1,4,3,128]{3,1,2,0:T(4,128)S(1)}, f32[1,4,3,128]{3,1,2,0:T(4,128)}, u32[]{:S(2)}) copy-start(f32[1,4,3,128]{3,1,2,0:T(4,128)} %param.22) | copy-start | bytes 18436
  33.6 91.6 %copy-start.2 = (f32[50,1,4,3,128]{4,2,3,1,0:T(4,128)S(1)}, f32[50,1,4,3,128]{4,2,3,1,0:T(4,128)}, u32[]{:S(2)}) copy-start(f32[50,1,4,3,128]{4,2,3,1,0:T(4,128)} %param.24) | copy-start | bytes 921604
  33.6 102.4 %copy-start.3 = (f32[64,3,128]{2,0,1:T(8,128)S(1)}, f32[64,3,128]{2,0,1:T(8,128)}, u32[]{:S(2)}) copy-start(f32[64,3,128]{2,0,1:T(8,128)} %param.15) | copy-start | bytes 294916
  33.6 102.4 %copy-start.4 = (f32[64,3,128]{2,0,1:T(8,128)S(1)}, f32[64,3,128]{2,0,1:T(8,128)}, u32[]{:S(2)}) copy-start(f32[64,3,128]{2,0,1:T(8,128)} %param.16) | copy-start | bytes 294916
  34.7 12.5 %all-to-all-start.2 = ((f32[16,8,3,128]{3,1,2,0:T(8,128)}), f32[16,8,3,128]{3,1,2,0:T(8,128)S(1)}, u32[]{:S(2)}, u32[]{:S(2)}) async-start(f32[16,8,3,128]{3,1,2,0:T(8,128)} %copy.45), calls=%async_computation.2 | async-start | bytes 393216 | tf_op jit(solution)/shard_map/all_to_all | solution.py:101
  138.8 12.5 %all-to-all-start.4 = ((f32[16,8,3,128]{3,1,2,0:T(8,128)}), f32[16,8,3,128]{3,1,2,0:T(8,128)S(1)}, u32[]{:S(2)}, u32[]{:S(2)}) async-start(f32[16,8,3,128]{3,1,2,0:T(8,128)} %copy.57), calls=%async_computation.4 | async-start | bytes 393216 | tf_op jit(solution)/shard_map/all_to_all | solution.py:101
  229.2 11.8 %copy-start.7 = (f32[1,4,3,128]{3,1,2,0:T(4,128)}, f32[1,4,3,128]{3,1,2,0:T(4,128)S(1)}, u32[]{:S(2)}) copy-start(f32[1,4,3,128]{3,1,2,0:T(4,128)S(1)} %copy_add_fusion) | copy-start | bytes 18436
